TPU v7x, 128 devices: a whole 4x4x4 slice. The times are simulated.
128 devices in a mesh: shell: 4 (over y_hi, core), img: 32 (over z, y_lo, x).
Axes of the slice: x: 4, y: 4 (y_hi: 2, y_lo: 2; y = y_hi * 2 + y_lo), z: 4, core: 2. Of those that a mesh axis runs over, the one named last changes fastest.
Arguments:
- images: bfloat16 [24576, 16384], P('img', 'shell'), may hold values from -12 to 12, as said below
- references: bfloat16 [1024, 16384], P('img', 'shell'), may hold values from -1 to 1, as said below
- shell_of_pixel: int32 [16384], P('shell'), may hold values from 0 to 63
- noise_power: float32 [64], replicated, may hold values from 0.1 to 10
- ref_class: int32 [1024], replicated, may hold values from 0 to 3
- ref_orient: int32 [1024], replicated, may hold values from 0 to 6143
- class_logw: float32 [4], replicated, may hold values from -4 to 4
- orient_logw: float32 [6144], replicated, may hold values from -4 to 4
Outputs:
- accumulators: float32 [1024, 16384], P('img', 'shell')
- evidence_logarithm: float32 [24576], P('img')
Inputs may be any that keep to these rules, and one draw needn't show every extreme that they name: `images`: images are real-valued Fourier data. `references`: references are real-valued projections.
All inputs are finite; a program needn't handle non-finite values.
Results may differ from a plain program's by a relative error of at most 0.0077.
Values may be sent and summed in bfloat16 or wider, within the bound.
A program may use at most 128 MiB of HBM per device.

v0:
```python
import jax
import jax.numpy as jnp
from jax import lax
from jax.sharding import PartitionSpec as P

inverse_heat_factor = 0.5


def split_up(array, dim, peers):
    dims = array.shape
    tiles = array.reshape(*dims[:dim], peers, dims[dim] // peers, *dims[dim + 1 :])
    return jnp.moveaxis(tiles, dim, 0)


def sum_at_owner(array, axis, dim):
    peers = lax.axis_size(axis)
    tiles = lax.all_to_all(split_up(array, dim, peers), axis, 0, 0, tiled=True)
    return jnp.sum(tiles, axis=0)


def sent_to_all(array, axis):
    peers = lax.axis_size(axis)
    return lax.all_to_all(
        jnp.broadcast_to(array[None], (peers, *array.shape)), axis, 0, 0, tiled=True
    )


def in_order(tiles, dim):
    dims = list(tiles.shape[1:])
    dims[dim] *= tiles.shape[0]
    return jnp.moveaxis(tiles, 0, dim).reshape(dims)


def gathered_copies(array, axis, dim):
    tiles = sent_to_all(array, axis)
    return in_order(tiles, dim)


def tempered_softmax(overall_total, beforehand_logarithmic_share):
    raw_logarithmic_measures = (
        inverse_heat_factor * overall_total + beforehand_logarithmic_share[None, :]
    )
    highest = jnp.max(raw_logarithmic_measures, axis=1)
    evidence_logarithm = highest + jnp.log(
        jnp.sum(jnp.exp(raw_logarithmic_measures - highest[:, None]), axis=1)
    )
    posterior = jnp.exp(raw_logarithmic_measures - evidence_logarithm[:, None]).astype(jnp.bfloat16)
    return (posterior, evidence_logarithm)


def shards(
    images, references, shell_of_pixel, noise_power, ref_class, ref_orient, class_logw, orient_logw
):
    inverse_noise = 1.0 / noise_power
    matches = shell_of_pixel[:, None] == jnp.arange(noise_power.shape[0], dtype=jnp.int32)[None, :]
    weights = jnp.sum(jnp.where(matches, inverse_noise[None, :], jnp.float32(0.0)), axis=1)
    weighted = (images.astype(jnp.float32) * weights[None, :]).astype(jnp.bfloat16)
    reference_block_list = lax.all_gather(references, "img", axis=0, tiled=True)
    correlation = lax.dot_general(
        weighted, reference_block_list, (((1,), (1,)), ((), ())), preferred_element_type=jnp.float32
    )
    block_float = reference_block_list.astype(jnp.float32)
    ref_norm = jnp.dot(block_float * block_float, weights, precision=lax.Precision.HIGHEST)
    incomplete_measures = correlation - 0.5 * ref_norm[None, :]
    class_agreement = (
        ref_class[:, None] == jnp.arange(class_logw.shape[0], dtype=jnp.int32)[None, :]
    )
    beforehand_logarithmic_share = (
        jnp.sum(jnp.where(class_agreement, class_logw[None, :], jnp.float32(0.0)), axis=1)
        + orient_logw[ref_orient]
    )
    score_rows = sum_at_owner(incomplete_measures, "shell", 0)
    row_posterior, row_log_marginal = tempered_softmax(score_rows, beforehand_logarithmic_share)
    posterior, evidence_logarithm = (
        gathered_copies(row_posterior, "shell", 0),
        gathered_copies(row_log_marginal.astype(jnp.bfloat16), "shell", 0).astype(
            row_log_marginal.dtype
        ),
    )
    accumulators = lax.psum_scatter(
        lax.dot_general(
            posterior, images, (((0,), (0,)), ((), ())), preferred_element_type=jnp.float32
        ),
        "img",
        scatter_dimension=0,
        tiled=True,
    )
    return (accumulators, evidence_logarithm)


def solution(mesh):
    placed = (P("img", "shell"), P("img", "shell"), P("shell"), P(), P(), P(), P(), P())
    return jax.shard_map(
        shards, mesh=mesh, in_specs=placed, out_specs=(P("img", "shell"), P("img")), check_vma=False
    )
```

profile of v0, /device:TPU:0, one launch (start us, length us, event | category | flops | bytes accessed | tf_op | source)
XLA Modules:
  0.0 501.9 jit_solution(11843192143524128233)
XLA Ops:
  7.2 0.0 copy-start
  7.2 0.0 all-gather.2.cloned.1.call-start
  7.2 0.7 all-gather.2.cloned.1.call-update
  7.9 0.7 broadcast_divide_fusion
  8.6 1.0 select_reduce_fusion
  9.5 168.8 %all-gather.2.cloned.1.call-done = bf16[1024,4096]{1,0:T(8,128)(2,1)} async-done(((bf16[32,4096]{1,0:T(8,128)(2,1)}), bf16[1024,4096]{1,0:T(8,128)(2,1)}) %all-gather.2.cloned.1.call-update) | async-done | bytes 8388624 | tf_op jit(solution)/shard_map/all_gather | solution.py:58
  178.3 18.0 %fusion = f32[1,1024]{1,0:T(1,128)S(1)} fusion(f32[4096,1]{0,1:T(1,128)S(1)} %bitcast.10, bf16[1024,4096]{1,0:T(8,128)(2,1)} %all-gather.2.cloned.1.call-done), kind=kOutput, calls=%fused_computation.1 | convolution fusion | flops 58720256 | bytes 8409088 | tf_op jit(solution)/shard_map/dot_general | solution.py:63
  196.3 0.0 copy-done.1
  196.4 10.3 %fusion.5 = f32[768,1024]{1,0:T(8,128)} fusion(bf16[1024,4096]{1,0:T(8,128)(2,1)S(1)} %copy-done.1, bf16[768,4096]{1,0:T(8,128)(2,1)} %param.8, f32[4096]{0:T(1024)S(1)} %select_reduce_fusion, f32[1024]{0:T(1024)S(1)} %broadcast_multiply_fusion), kind=kOutput, calls=%fused_computation.7 | convolution fusion | flops 6452674560 | bytes 17846272 | tf_op jit(solution)/shard_map/dot_general | solution.py:59
  206.6 4.3 all-to-all-start
  210.9 6.2 %gather_fusion = f32[1024]{0:T(1024)S(1)} fusion(f32[6144]{0:T(1024)S(1)} %copy-done, s32[1024]{0:T(1024)S(1)} %fusion.7), kind=kCustom, calls=%fused_computation | custom fusion | bytes 12288 | tf_op jit(solution)/shard_map/gather | solution.py:70
  217.1 0.1 select_reduce_fusion.1
  217.2 32.1 %all-to-all-done = f32[4,192,1024]{2,1,0:T(8,128)S(1)} async-done(((f32[4,192,1024]{2,1,0:T(8,128)}), f32[4,192,1024]{2,1,0:T(8,128)S(1)}, u32[]{:S(2)}, u32[]{:S(2)}) %all-to-all-start) | async-done | bytes 3145760 | tf_op jit(solution)/shard_map/all_to_all | solution.py:17
  249.3 1.2 reduce_sum.37
  250.5 1.3 fusion.6
  251.8 1.4 exponential_reduce_fusion
  253.2 1.3 exponential_convert_fusion
  254.6 0.2 broadcast_in_dim.35
  254.8 24.0 %all_to_all.16 = bf16[4,192,1024]{2,1,0:T(8,128)(2,1)S(1)} all-to-all(bf16[4,192,1024]{2,1,0:T(8,128)(2,1)S(1)} %broadcast_in_dim.35), channel_id=1, replica_groups=mesh['shell'=4,'img'=32] {'shell'}, dimensions={0} | all-to-all | bytes 3145728 | tf_op jit(solution)/shard_map/all_to_all | solution.py:23
  278.8 13.0 %fusion.9 = f32[1024,4096]{1,0:T(8,128)} fusion(bf16[768,1024]{1,0:T(8,128)(2,1)S(1)} %bitcast.8, bf16[768,4096]{1,0:T(8,128)(2,1)} %param.8), kind=kOutput, calls=%fused_computation.23 | convolution fusion | flops 6442450944 | bytes 24641536 | tf_op jit(solution)/shard_map/dot_general | solution.py:81
  291.8 0.0 reduce-scatter.2.cloned.1.call-update
  291.8 7.6 %all_to_all.17 = bf16[4,1,192]{2,1,0:T(2,128)(2,1)S(1)} all-to-all(bf16[4,1,192]{2,1,0:T(2,128)(2,1)S(1)} %broadcast_in_dim.56), channel_id=1, replica_groups=mesh['shell'=4,'img'=32] {'shell'}, dimensions={0} | all-to-all | bytes 3072 | tf_op jit(solution)/shard_map/all_to_all | solution.py:23
  299.5 0.7 reshape.81
  300.2 194.9 %reduce-scatter.2.cloned.1.call-done = f32[32,4096]{1,0:T(8,128)} async-done(((f32[1024,4096]{1,0:T(8,128)}), f32[32,4096]{1,0:T(8,128)}) %reduce-scatter.2.cloned.1.call-update) | async-done | bytes 524304 | tf_op jit(solution)/shard_map/reduce_scatter | solution.py:80
  (15 shorter events, 0.1 us)
Async XLA Ops:
  7.2 203.7 %copy-start = (f32[6144]{0:T(1024)S(1)}, f32[6144]{0:T(1024)}, u32[]{:S(2)}) copy-start(f32[6144]{0:T(1024)} %param.15) | copy-start | bytes 73732
  7.2 171.1 %all-gather.2.cloned.1.call-start = ((), (), s32[]{:S(2)}) async-start(), calls=%async_computation.4 | async-start | bytes 8650752 | tf_op jit(solution)/shard_map/all_gather | solution.py:58
  178.3 18.0 %copy-start.1 = (bf16[1024,4096]{1,0:T(8,128)(2,1)S(1)}, bf16[1024,4096]{1,0:T(8,128)(2,1)}, u32[]{:S(2)}) copy-start(bf16[1024,4096]{1,0:T(8,128)(2,1)} %all-gather.2.cloned.1.call-done) | copy-start | bytes 25165828
  206.6 4.3 copy-start.2
  206.6 10.5 %copy-start.3 = (s32[1024]{0:T(1024)S(1)}, s32[1024]{0:T(1024)}, u32[]{:S(2)}) copy-start(s32[1024]{0:T(1024)} %param.12) | copy-start | bytes 12292
  206.6 10.5 %copy-start.4 = (f32[4]{0:T(128)S(1)}, f32[4]{0:T(128)}, u32[]{:S(2)}) copy-start(f32[4]{0:T(128)} %param.14) | copy-start | bytes 52
  206.6 42.7 %all-to-all-start = ((f32[4,192,1024]{2,1,0:T(8,128)}), f32[4,192,1024]{2,1,0:T(8,128)S(1)}, u32[]{:S(2)}, u32[]{:S(2)}) async-start(f32[4,192,1024]{2,1,0:T(8,128)} %bitcast.9), calls=%async_computation | async-start | bytes 6291456 | tf_op jit(solution)/shard_map/all_to_all | solution.py:17
  210.9 284.2 %reduce-scatter.2.cloned.1.call-start = ((), (), s32[]{:S(2)}) async-start(), calls=%async_computation.5 | async-start | bytes 17301504 | tf_op jit(solution)/shard_map/reduce_scatter | solution.py:80
Sparse Core Ops, SparseCore 0:
  9.6 168.6 all-gather.1
  291.9 203.1 reduce-scatter.1
where the time goes:
time: 502 us
  waiting for transfers between devices  397 us (79%)
  matrix products  41.3 us (8%)
  blocking collectives  31.6 us (6%)
  between operations  14.1 us (3%)
  local copies, waits for them, and re-layouts  7.06 us (1%)
  other arithmetic  6.99 us (1%)
    reduce_scatter x1, waiting for transfers between devices, shards(): lax.psum_scatter(lax.dot_general(posterior, images, (((0,), (0,)), ((), (...  195 us
    all_gather x1, waiting for transfers between devices, shards(): reference_block_list = lax.all_gather(references, 'img', axis=0, tiled=True)  169 us
    all_to_all x1, waiting for transfers between devices, sum_at_owner(): tiles = lax.all_to_all(split_up(array, dim, peers), axis, 0, 0, tiled=True)  32.1 us
    all_to_all x2, blocking collectives, sent_to_all(): lax.all_to_all(jnp.broadcast_to(array[None], (peers, *array.shape)), axis...  31.6 us
    dot_general x1, matrix products, shards(): jnp.dot(block_float * block_float, weights, precision=lax.Precision.HIGHEST)  18 us
    dot_general x1, matrix products, shards(): lax.dot_general(posterior, images, (((0,), (0,)), ((), ())), preferred_el...  13 us
    dot_general x1, matrix products, shards(): lax.dot_general(weighted, reference_block_list, (((1,), (1,)), ((), ())),...  10.3 us
  transfers between devices with their start and end apart: 3, of which 3 were waited for; matrix products, arithmetic and copies ran while one was open for 2% of the time, Pallas kernels for 0%

commit v1 on v0

--- a/solution.py
+++ b/solution.py
@@ -55,7 +55,9 @@
     matches = shell_of_pixel[:, None] == jnp.arange(noise_power.shape[0], dtype=jnp.int32)[None, :]
     weights = jnp.sum(jnp.where(matches, inverse_noise[None, :], jnp.float32(0.0)), axis=1)
     weighted = (images.astype(jnp.float32) * weights[None, :]).astype(jnp.bfloat16)
-    reference_block_list = lax.all_gather(references, "img", axis=0, tiled=True)
+    reference_block_list = jnp.concatenate(
+        lax.all_to_all(jnp.stack([references] * lax.axis_size("img")), "img", 0, 0), axis=0
+    )
     correlation = lax.dot_general(
         weighted, reference_block_list, (((1,), (1,)), ((), ())), preferred_element_type=jnp.float32
     )

time: 502 us -> 469 us (0.934)
  waiting for transfers between devices: 397 us -> 348 us
  starting transfers between devices: 4.3 us -> 13.9 us
  local copies, waits for them, and re-layouts: 7.06 us -> 12.3 us
    all_gather x1 -> x0, waiting for transfers between devices: 169 us -> none  [shards(): reference_block_list = lax.all_gather(references, 'img', axis=0, tiled=True)]
    all_to_all x0 -> x1, waiting for transfers between devices: none -> 119 us  [shards(): lax.all_to_all(jnp.stack([references] * lax.axis_size('img')), 'img', 0, 0)]
    all_to_all x0 -> x1, starting transfers between devices: none -> 9.55 us  [shards(): lax.all_to_all(jnp.stack([references] * lax.axis_size('img')), 'img', 0, 0)]
    another operation x0 -> x1, local copies, waits for them, and re-layouts: none -> 5.21 us  [shards(): jnp.stack([references] * lax.axis_size('img'))]
where the time goes in v1:
time: 469 us
  waiting for transfers between devices  348 us (74%)
  matrix products  42.5 us (9%)
  blocking collectives  31.6 us (7%)
  between operations  14.1 us (3%)
  starting transfers between devices  13.9 us (3%)
  local copies, waits for them, and re-layouts  12.3 us (3%)
  other arithmetic  5.62 us (1%)
    reduce_scatter x1, waiting for transfers between devices, shards(): lax.psum_scatter(lax.dot_general(posterior, images, (((0,), (0,)), ((), (...  197 us
    all_to_all x1, waiting for transfers between devices, shards(): lax.all_to_all(jnp.stack([references] * lax.axis_size('img')), 'img', 0, 0)  119 us
    all_to_all x1, waiting for transfers between devices, sum_at_owner(): tiles = lax.all_to_all(split_up(array, dim, peers), axis, 0, 0, tiled=True)  32.1 us
    all_to_all x2, blocking collectives, sent_to_all(): lax.all_to_all(jnp.broadcast_to(array[None], (peers, *array.shape)), axis...  31.6 us
    dot_general x1, matrix products, shards(): jnp.dot(block_float * block_float, weights, precision=lax.Precision.HIGHEST)  17.3 us
    dot_general x1, matrix products, shards(): lax.dot_general(posterior, images, (((0,), (0,)), ((), ())), preferred_el...  13 us
    dot_general x1, matrix products, shards(): lax.dot_general(weighted, reference_block_list, (((1,), (1,)), ((), ())),...  12.2 us
    all_to_all x1, starting transfers between devices, shards(): lax.all_to_all(jnp.stack([references] * lax.axis_size('img')), 'img', 0, 0)  9.55 us
  transfers between devices with their start and end apart: 3, of which 3 were waited for; matrix products, arithmetic and copies ran while one was open for 2% of the time, Pallas kernels for 0%

profile of v1, /device:TPU:0, one launch (start us, length us, event | category | flops | bytes accessed | tf_op | source)
XLA Modules:
  0.0 468.5 jit_solution(17333248540586792509)
XLA Ops:
  7.2 0.0 copy-start
  7.2 5.2 %stack.2 = bf16[32,32,4096]{2,1,0:T(8,128)(2,1)} broadcast(bf16[32,4096]{1,0:T(8,128)(2,1)} %param.9), dimensions={1,2} | broadcast | bytes 8650752 | tf_op jit(solution)/shard_map/stack | solution.py:59
  12.4 9.5 %all-to-all-start = ((bf16[32,32,4096]{2,1,0:T(8,128)(2,1)}), bf16[32,32,4096]{2,1,0:T(8,128)(2,1)}, u32[]{:S(2)}, u32[]{:S(2)}) async-start(bf16[32,32,4096]{2,1,0:T(8,128)(2,1)} %stack.2), calls=%async_computation | async-start | bytes 16777216 | tf_op jit(solution)/shard_map/all_to_all | solution.py:59
  21.9 0.0 copy-done.5
  22.0 0.2 select_reduce_fusion
  22.2 119.3 %all-to-all-done = bf16[32,32,4096]{2,1,0:T(8,128)(2,1)} async-done(((bf16[32,32,4096]{2,1,0:T(8,128)(2,1)}), bf16[32,32,4096]{2,1,0:T(8,128)(2,1)}, u32[]{:S(2)}, u32[]{:S(2)}) %all-to-all-start) | async-done | bytes 8388640 | tf_op jit(solution)/shard_map/all_to_all | solution.py:59
  141.5 17.3 %fusion = f32[1,1024]{1,0:T(1,128)S(1)} fusion(f32[4096,1]{0,1:T(1,128)S(1)} %bitcast.11, bf16[1024,4096]{1,0:T(8,128)(2,1)} %bitcast), kind=kOutput, calls=%fused_computation.1 | convolution fusion | flops 58720256 | bytes 8409088 | tf_op jit(solution)/shard_map/dot_general | solution.py:65
  158.7 12.2 %fusion.5 = f32[768,1024]{1,0:T(8,128)} fusion(bf16[1024,4096]{1,0:T(8,128)(2,1)} %bitcast, bf16[768,4096]{1,0:T(8,128)(2,1)} %param.8, f32[4096]{0:T(1024)S(1)} %select_reduce_fusion, f32[1024]{0:T(1024)S(1)} %broadcast_multiply_fusion), kind=kOutput, calls=%fused_computation.7 | convolution fusion | flops 6452674560 | bytes 17846272 | tf_op jit(solution)/shard_map/dot_general | solution.py:61
  171.0 4.3 all-to-all-start.1
  175.3 0.0 reduce-scatter.2.cloned.1.call-start
  175.3 6.2 %gather_fusion = f32[1024]{0:T(1024)S(1)} fusion(f32[6144]{0:T(1024)S(1)} %copy-done, s32[1024]{0:T(1024)S(1)} %fusion.7), kind=kCustom, calls=%fused_computation | custom fusion | bytes 12288 | tf_op jit(solution)/shard_map/gather | solution.py:72
  181.5 0.1 select_reduce_fusion.1
  181.6 32.1 %all-to-all-done.1 = f32[4,192,1024]{2,1,0:T(8,128)S(1)} async-done(((f32[4,192,1024]{2,1,0:T(8,128)}), f32[4,192,1024]{2,1,0:T(8,128)S(1)}, u32[]{:S(2)}, u32[]{:S(2)}) %all-to-all-start.1) | async-done | bytes 3145760 | tf_op jit(solution)/shard_map/all_to_all | solution.py:17
  213.7 1.2 reduce_sum.37
  214.9 1.3 fusion.6
  216.2 1.4 exponential_reduce_fusion
  217.6 1.3 exponential_convert_fusion
  219.0 0.2 broadcast_in_dim.35
  219.2 24.0 %all_to_all.21 = bf16[4,192,1024]{2,1,0:T(8,128)(2,1)S(1)} all-to-all(bf16[4,192,1024]{2,1,0:T(8,128)(2,1)S(1)} %broadcast_in_dim.35), channel_id=1, replica_groups=mesh['shell'=4,'img'=32] {'shell'}, dimensions={0} | all-to-all | bytes 3145728 | tf_op jit(solution)/shard_map/all_to_all | solution.py:23
  243.2 13.0 %fusion.9 = f32[1024,4096]{1,0:T(8,128)} fusion(bf16[768,1024]{1,0:T(8,128)(2,1)S(1)} %bitcast.9, bf16[768,4096]{1,0:T(8,128)(2,1)} %param.8), kind=kOutput, calls=%fused_computation.23 | convolution fusion | flops 6442450944 | bytes 24641536 | tf_op jit(solution)/shard_map/dot_general | solution.py:83
  256.2 0.0 reduce-scatter.2.cloned.1.call-update
  256.2 7.6 %all_to_all.22 = bf16[4,1,192]{2,1,0:T(2,128)(2,1)S(1)} all-to-all(bf16[4,1,192]{2,1,0:T(2,128)(2,1)S(1)} %broadcast_in_dim.56), channel_id=1, replica_groups=mesh['shell'=4,'img'=32] {'shell'}, dimensions={0} | all-to-all | bytes 3072 | tf_op jit(solution)/shard_map/all_to_all | solution.py:23
  263.9 0.7 reshape.87
  264.6 197.1 %reduce-scatter.2.cloned.1.call-done = f32[32,4096]{1,0:T(8,128)} async-done(((f32[1024,4096]{1,0:T(8,128)}), f32[32,4096]{1,0:T(8,128)}) %reduce-scatter.2.cloned.1.call-update) | async-done | bytes 524304 | tf_op jit(solution)/shard_map/reduce_scatter | solution.py:82
  (17 shorter events, 0.1 us)
Async XLA Ops:
  7.2 168.2 %copy-start = (f32[6144]{0:T(1024)S(1)}, f32[6144]{0:T(1024)}, u32[]{:S(2)}) copy-start(f32[6144]{0:T(1024)} %param.15) | copy-start | bytes 73732
  12.4 9.6 %copy-start.5 = (f32[64]{0:T(128)S(1)}, f32[64]{0:T(128)}, u32[]{:S(2)}) copy-start(f32[64]{0:T(128)} %param.11) | copy-start | bytes 772
  12.4 9.6 %copy-start.1 = (s32[4096]{0:T(1024)S(1)}, s32[4096]{0:T(1024)}, u32[]{:S(2)}) copy-start(s32[4096]{0:T(1024)} %param.10) | copy-start | bytes 49156
  12.4 129.1 %all-to-all-start = ((bf16[32,32,4096]{2,1,0:T(8,128)(2,1)}), bf16[32,32,4096]{2,1,0:T(8,128)(2,1)}, u32[]{:S(2)}, u32[]{:S(2)}) async-start(bf16[32,32,4096]{2,1,0:T(8,128)(2,1)} %stack.2), calls=%async_computation | async-start | bytes 16777216 | tf_op jit(solution)/shard_map/all_to_all | solution.py:59
  171.0 4.3 copy-start.2
  171.0 10.5 %copy-start.3 = (s32[1024]{0:T(1024)S(1)}, s32[1024]{0:T(1024)}, u32[]{:S(2)}) copy-start(s32[1024]{0:T(1024)} %param.12) | copy-start | bytes 12292
  171.0 10.5 %copy-start.4 = (f32[4]{0:T(128)S(1)}, f32[4]{0:T(128)}, u32[]{:S(2)}) copy-start(f32[4]{0:T(128)} %param.14) | copy-start | bytes 52
  171.0 42.7 %all-to-all-start.1 = ((f32[4,192,1024]{2,1,0:T(8,128)}), f32[4,192,1024]{2,1,0:T(8,128)S(1)}, u32[]{:S(2)}, u32[]{:S(2)}) async-start(f32[4,192,1024]{2,1,0:T(8,128)} %bitcast.10), calls=%async_computation.1 | async-start | bytes 6291456 | tf_op jit(solution)/shard_map/all_to_all | solution.py:17
  175.3 286.4 %reduce-scatter.2.cloned.1.call-start = ((), (), s32[]{:S(2)}) async-start(), calls=%async_computation.5 | async-start | bytes 17301504 | tf_op jit(solution)/shard_map/reduce_scatter | solution.py:82
Sparse Core Ops, SparseCore 0:
  256.4 205.2 reduce-scatter.1
